TPU v7x, 32 devices: a whole 2x2x4 slice. The times are simulated.
32 devices in a mesh: gx: 2 (over x), gy: 4 (over y, core), gz: 4 (over z).
Axes of the slice: x: 2, y: 2, z: 4, core: 2. Of those that a mesh axis runs over, the one named last changes fastest.
Arguments:
- fields: float32 [6, 32, 64, 512], P(None, 'gx', 'gy', 'gz'), may hold values from -6 to 6
- permittivity: float32 [32, 64, 512], P('gx', 'gy', 'gz'), may hold values from 1 to 4
- donor_owner: int32 [4096, 1], P(('gx', 'gy', 'gz')), may hold values from 0 to 15; in each aligned block of 128 rows (0 to 127, 128 to 255, ...) at most 16 rows name the same one
- donor_base: int32 [4096, 3], P(('gx', 'gy', 'gz')), may hold values from 0 to 127, as said below
- donor_weights: float32 [4096, 15], P(('gx', 'gy', 'gz')), may hold values from -3 to 3
Outputs:
- new_fields: float32 [6, 32, 64, 512], P(None, 'gx', 'gy', 'gz')
- receptor_values: float32 [6, 4096], P(None, ('gx', 'gy', 'gz'))
Inputs may be any that keep to these rules, and one draw needn't show every extreme that they name: `donor_owner`: within the 128 rows of one device no owner index is named by more than 16 rows, and one is named by exactly 16. `donor_base`: column 0 lies in 0 to 15, column 1 in 0 to 15, column 2 in 0 to 127.
All inputs are finite; a program needn't handle non-finite values.
Results may differ from a plain program's by a relative error of at most 0.00002.
Values sent between devices are 32-bit elements; how exact they have to be, the bound alone decides.
A program may use at most 192 MiB of HBM per device.

v0:
```python
import jax
import jax.numpy as jnp
from jax import lax
from jax.sharding import PartitionSpec as P

step_size = 0.25


def padded_2(cells, sides, width):
    for axis, dim in sides:
        count = lax.axis_size(axis)
        ends = count - 1
        head = lax.slice_in_dim(cells, 0, width, axis=dim)
        tail = lax.slice_in_dim(cells, cells.shape[dim] - width, cells.shape[dim], axis=dim)
        cells = jnp.concatenate(
            [
                lax.ppermute(tail, axis, [(i, (i + 1) % count) for i in range(ends)]),
                cells,
                lax.ppermute(head, axis, [((i + 1) % count, i) for i in range(ends)]),
            ],
            axis=dim,
        )
    return cells


def shifted(field, axis_index, offset):
    window = [slice(2, -2), slice(2, -2), slice(2, -2)]
    length = field.shape[axis_index] - 4
    window[axis_index] = slice(2 + offset, 2 + offset + length)
    return field[tuple(window)]


def derivative(field, axis_index):
    outer = shifted(field, axis_index, -2) - shifted(field, axis_index, 2)
    inner = shifted(field, axis_index, 1) - shifted(field, axis_index, -1)
    return (outer + 8.0 * inner) / 12.0


def curl_rate(padded, coefficient):
    rate_ex = (derivative(padded[5], 1) - derivative(padded[4], 2)) / coefficient
    rate_ey = (derivative(padded[3], 2) - derivative(padded[5], 0)) / coefficient
    rate_ez = (derivative(padded[4], 0) - derivative(padded[3], 1)) / coefficient
    rate_hx = derivative(padded[1], 2) - derivative(padded[2], 1)
    rate_hy = derivative(padded[2], 0) - derivative(padded[0], 2)
    rate_hz = derivative(padded[0], 1) - derivative(padded[1], 0)
    return jnp.stack([rate_ex, rate_ey, rate_ez, rate_hx, rate_hy, rate_hz])


def contract(donor_tiles, weights):
    weight_x = weights[0:5]
    weight_y = weights[5:10]
    weight_z = weights[10:15]
    along_z = jnp.sum(donor_tiles * weight_z[None, None, None, :, :], axis=3)
    along_y = jnp.sum(along_z * weight_y[None, None, :, :], axis=2)
    return jnp.sum(along_y * weight_x[None, :, :], axis=1)


def gather_tiles(donor_grid, corner_rows):
    components, extent_x, extent_y, extent_z = donor_grid.shape
    flat_grid = donor_grid.reshape(components, extent_x * extent_y * extent_z)
    stencil = jnp.arange(5, dtype=jnp.int32)
    offsets = (
        stencil[:, None, None] * (extent_y * extent_z)
        + stencil[None, :, None] * extent_z
        + stencil[None, None, :]
    ).reshape(125)
    starts = corner_rows[0] * (extent_y * extent_z) + corner_rows[1] * extent_z + corner_rows[2]
    picked = jnp.take(flat_grid, offsets[:, None] + starts[None, :], axis=1)
    return picked.reshape(components, 5, 5, 5, corner_rows.shape[1])


def place_rims(extended, along):
    widths = [(2, 2), (2, 2), (2, 2)]
    widths[along] = (0, 0)
    return jnp.pad(extended, widths)


def assemble(first_ext, first_axis, second_ext, second_axis):
    full_first = place_rims(first_ext, first_axis)
    full_second = place_rims(second_ext, second_axis)
    length = full_first.shape[first_axis]
    position = jnp.arange(length, dtype=jnp.int32)
    interior = (position >= 2) & (position < length - 2)
    shape = [1, 1, 1]
    shape[first_axis] = length
    return jnp.where(interior.reshape(shape), full_second, full_first)


def local(fields, permittivity, donor_owner, donor_base, donor_weights):
    accumulated = fields
    taylor_term = fields
    for power in range(1, 5):
        x_rims = padded_2(taylor_term[jnp.array([1, 2, 4, 5])], (("gx", 1),), 2)
        y_rims = padded_2(taylor_term[jnp.array([0, 2, 3, 5])], (("gy", 2),), 2)
        z_rims = padded_2(taylor_term[jnp.array([0, 1, 3, 4])], (("gz", 3),), 2)
        padded = jnp.stack(
            [
                assemble(y_rims[0], 1, z_rims[0], 2),
                assemble(x_rims[0], 0, z_rims[1], 2),
                assemble(x_rims[1], 0, y_rims[1], 1),
                assemble(y_rims[2], 1, z_rims[2], 2),
                assemble(x_rims[2], 0, z_rims[3], 2),
                assemble(x_rims[3], 0, y_rims[3], 1),
            ]
        )
        taylor_term = step_size / power * curl_rate(padded, permittivity)
        accumulated = accumulated + taylor_term
    donor_grid = padded_2(accumulated, (("gx", 1), ("gy", 2), ("gz", 3)), 2)
    group_size = lax.axis_size("gy") * lax.axis_size("gz")
    row_count = donor_owner.shape[0]
    capacity = 2 * row_count // group_size
    owner_id = donor_owner[:, 0]
    owner_hits = (owner_id[:, None] == jnp.arange(group_size, dtype=jnp.int32)[None, :]).astype(
        jnp.int32
    )
    earlier = jnp.cumsum(owner_hits, axis=0) - owner_hits
    slot_index = jnp.sum(earlier * owner_hits, axis=1)
    flat_index = owner_id * capacity + slot_index
    corner_send = (
        jnp.zeros((3, group_size * capacity), jnp.int32).at[:, flat_index].set(donor_base.T)
    )
    corner_send = corner_send.reshape(3, group_size, capacity)
    weight_send = (
        jnp.zeros((15, group_size * capacity), jnp.float32).at[:, flat_index].set(donor_weights.T)
    )
    weight_send = weight_send.reshape(15, group_size, capacity)
    donor_corners = lax.all_to_all(
        corner_send, ("gy", "gz"), split_axis=1, concat_axis=1, tiled=True
    )
    slot_count = donor_corners.shape[2]
    donor_tiles = gather_tiles(donor_grid, donor_corners.reshape(3, -1))
    returned = lax.all_to_all(
        donor_tiles.reshape(750, group_size, slot_count),
        ("gy", "gz"),
        split_axis=1,
        concat_axis=1,
        tiled=True,
    )
    answers = contract(returned.reshape(6, 5, 5, 5, -1), weight_send.reshape(15, -1))
    answers = answers.reshape(6, group_size, capacity)
    receptor_values = answers.reshape(6, -1)[:, flat_index]
    return (accumulated, receptor_values)


def solution(mesh):
    placed = (
        P(None, "gx", "gy", "gz"),
        P("gx", "gy", "gz"),
        P(("gx", "gy", "gz"), None),
        P(("gx", "gy", "gz"), None),
        P(("gx", "gy", "gz"), None),
    )
    return jax.shard_map(
        local,
        mesh=mesh,
        in_specs=placed,
        out_specs=(P(None, "gx", "gy", "gz"), P(None, ("gx", "gy", "gz"))),
        check_vma=False,
    )
```

profile of v0, /device:TPU:0, one launch (start us, length us, event | category | flops | bytes accessed | tf_op | source)
XLA Modules:
  0.0 321.4 jit_solution(8976261912518652279)
XLA Ops:
  4.4 1.7 gather_fusion
  6.2 2.4 collective-permute-start
  11.7 4.3 %collective-permute-start.4 = (f32[4,16,16,2]{3,2,1,0:T(8,128)}, f32[4,16,16,2]{3,2,1,0:T(8,128)S(1)}, u32[]{:S(2)}, u32[]{:S(2)}) collective-permute-start(f32[4,16,16,2]{3,2,1,0:T(8,128)} %get-tuple-element.88), channel_id=1, source_target_pairs={{0,1},{1,2},{2,3},{4,5},{5,6},{6,7},{8,9},{9,10},{10,11},{12,13},{... | collective-permute-start | bytes 24584 | tf_op jit(solution)/shard_map/ppermute | solution.py:17
  17.9 3.4 %collective-permute-start.2 = (f32[4,2,16,128]{3,2,1,0:T(8,128)S(1)}, f32[4,2,16,128]{3,2,1,0:T(8,128)S(1)}, u32[]{:S(2)}, u32[]{:S(2)}) collective-permute-start(f32[4,2,16,128]{3,2,1,0:T(8,128)S(1)} %get-tuple-element.91), channel_id=1, source_target_pairs={{0,16},{1,17},{2,18},{3,19},{4,20},{5,21},{6,22},{7,23},{8,24},{9,... | collective-permute-start | bytes 196616 | tf_op jit(solution)/shard_map/ppermute | solution.py:17
  23.1 10.3 %all-to-all-start = ((s32[3,16,16]{2,0,1:T(4,128)}), s32[3,16,16]{2,0,1:T(4,128)S(1)}, u32[]{:S(2)}, u32[]{:S(2)}) async-start(s32[3,16,16]{2,0,1:T(4,128)} %copy.91), calls=%async_computation | async-start | bytes 65536 | tf_op jit(solution)/shard_map/all_to_all | solution.py:127
  34.2 5.7 %all-to-all-done = s32[3,16,16]{2,0,1:T(4,128)S(1)} async-done(((s32[3,16,16]{2,0,1:T(4,128)}), s32[3,16,16]{2,0,1:T(4,128)S(1)}, u32[]{:S(2)}, u32[]{:S(2)}) %all-to-all-start) | async-done | bytes 3104 | tf_op jit(solution)/shard_map/all_to_all | solution.py:127
  41.4 1.5 pad_maximum_fusion.2
  43.2 3.0 collective-permute-done.3
  49.3 1.5 gather_fusion.4
  51.4 1.4 gather_fusion.3
  53.8 1.6 collective-permute-start.8
  56.9 2.4 collective-permute-start.10
  61.9 8.2 %collective-permute-done.10 = f32[4,16,16,2]{3,2,1,0:T(8,128)S(1)} collective-permute-done((f32[4,16,16,2]{3,2,1,0:T(8,128)S(1)}, f32[4,16,16,2]{3,2,1,0:T(8,128)S(1)}, u32[]{:S(2)}, u32[]{:S(2)}) %collective-permute-start.10) | collective-permute-done | bytes 8224 | tf_op jit(solution)/shard_map/ppermute | solution.py:17
  71.4 2.9 collective-permute-done.11
  80.0 1.5 gather_fusion.7
  82.1 1.4 gather_fusion.6
  84.4 4.3 %collective-permute-start.14 = (f32[4,2,16,128]{3,2,1,0:T(8,128)S(1)}, f32[4,2,16,128]{3,2,1,0:T(8,128)S(1)}, u32[]{:S(2)}, u32[]{:S(2)}) collective-permute-start(f32[4,2,16,128]{3,2,1,0:T(8,128)S(1)} %get-tuple-element.79), channel_id=1, source_target_pairs={{0,16},{1,17},{2,18},{3,19},{4,20},{5,21},{6,22},{7,23},{8,24},{9,... | collective-permute-start | bytes 196616 | tf_op jit(solution)/shard_map/ppermute | solution.py:17
  90.2 2.6 collective-permute-start.16
  94.2 1.9 collective-permute-start.12
  96.1 8.3 %collective-permute-done.16 = f32[4,16,16,2]{3,2,1,0:T(8,128)S(1)} collective-permute-done((f32[4,16,16,2]{3,2,1,0:T(8,128)S(1)}, f32[4,16,16,2]{3,2,1,0:T(8,128)S(1)}, u32[]{:S(2)}, u32[]{:S(2)}) %collective-permute-start.16) | collective-permute-done | bytes 8224 | tf_op jit(solution)/shard_map/ppermute | solution.py:17
  104.4 1.5 collective-permute-start.13
  105.9 2.7 collective-permute-done.17
  114.4 1.5 gather_fusion.10
  116.5 1.4 gather_fusion.9
  118.8 4.3 %collective-permute-start.20 = (f32[4,2,16,128]{3,2,1,0:T(8,128)S(1)}, f32[4,2,16,128]{3,2,1,0:T(8,128)S(1)}, u32[]{:S(2)}, u32[]{:S(2)}) collective-permute-start(f32[4,2,16,128]{3,2,1,0:T(8,128)S(1)} %get-tuple-element.73), channel_id=1, source_target_pairs={{0,16},{1,17},{2,18},{3,19},{4,20},{5,21},{6,22},{7,23},{8,24},{9,... | collective-permute-start | bytes 196616 | tf_op jit(solution)/shard_map/ppermute | solution.py:17
  124.6 2.6 collective-permute-start.22
  128.5 2.1 collective-permute-start.18
  130.6 8.3 %collective-permute-done.22 = f32[4,16,16,2]{3,2,1,0:T(8,128)S(1)} collective-permute-done((f32[4,16,16,2]{3,2,1,0:T(8,128)S(1)}, f32[4,16,16,2]{3,2,1,0:T(8,128)S(1)}, u32[]{:S(2)}, u32[]{:S(2)}) %collective-permute-start.22) | collective-permute-done | bytes 8224 | tf_op jit(solution)/shard_map/ppermute | solution.py:17
  140.2 2.9 collective-permute-done.23
  148.9 4.3 %collective-permute-start.24 = (f32[6,2,16,128]{3,2,1,0:T(8,128)S(1)}, f32[6,2,16,128]{3,2,1,0:T(8,128)S(1)}, u32[]{:S(2)}, u32[]{:S(2)}) collective-permute-start(f32[6,2,16,128]{3,2,1,0:T(8,128)S(1)} %get-tuple-element.34), channel_id=1, source_target_pairs={{0,16},{1,17},{2,18},{3,19},{4,20},{5,21},{6,22},{7,23},{8,24},{9,... | collective-permute-start | bytes 294920 | tf_op jit(solution)/shard_map/ppermute | solution.py:17
  155.4 4.3 %collective-permute-done.25 = f32[6,2,16,128]{3,2,1,0:T(8,128)S(1)} collective-permute-done((f32[6,2,16,128]{3,2,1,0:T(8,128)S(1)}, f32[6,2,16,128]{3,2,1,0:T(8,128)S(1)}, u32[]{:S(2)}, u32[]{:S(2)}) %collective-permute-start.25) | collective-permute-done | bytes 98336 | tf_op jit(solution)/shard_map/ppermute | solution.py:19
  159.8 1.3 collective-permute-start.26
  162.4 1.9 collective-permute-done.27
  164.6 1.6 fusion.240
  166.2 2.3 copy.92
  168.5 3.7 %collective-permute-start.28 = (f32[6,20,20,2]{2,1,3,0:T(8,128)S(1)}, f32[6,20,20,2]{2,1,3,0:T(8,128)S(1)}, u32[]{:S(2)}, u32[]{:S(2)}) collective-permute-start(f32[6,20,20,2]{2,1,3,0:T(8,128)S(1)} %copy.92), channel_id=1, source_target_pairs={{0,1},{1,2},{2,3},{4,5},{5,6},{6,7},{8,9},{9,10},{10,11},{12,13},{... | collective-permute-start | bytes 57608 | tf_op jit(solution)/shard_map/ppermute | solution.py:17
  173.2 1.5 collective-permute-start.29
  175.7 4.5 %collective-permute-done.29 = f32[6,20,20,2]{2,1,3,0:T(8,128)S(1)} collective-permute-done((f32[6,20,20,2]{2,1,3,0:T(8,128)S(1)}, f32[6,20,20,2]{2,1,3,0:T(8,128)S(1)}, u32[]{:S(2)}, u32[]{:S(2)}) %collective-permute-start.29) | collective-permute-done | bytes 19232 | tf_op jit(solution)/shard_map/ppermute | solution.py:19
  180.2 1.9 copy.95
  182.2 4.7 %pad_maximum_fusion = f32[6,20,20,132]{3,2,1,0:T(8,128)} fusion(f32[6,20,20,2]{3,2,1,0:T(8,128)} %copy.95, f32[6,20,2,128]{3,2,1,0:T(2,128)S(1)} %collective-permute-done.27, f32[6,2,16,128]{3,2,1,0:T(8,128)S(1)} %collective-permute-done.25, f32[6,16,16,128]{3,2,1,0:T(8,128)S(1)} %multiply_add_fusion, f32[6,2,16,128]{3,2,1,0:T(8,128)S(1)} %collective-permute-done.24, ...), kind=kLoop, calls=%fused_computation.16 | loop fusion | flops 1900800 | bytes 2534400 | tf_op jit(solution)/shard_map/concatenate | solution.py:15
  186.8 3.3 %reshape.217 = f32[6,52800]{1,0:T(8,128)S(1)} reshape(f32[6,20,20,132]{3,2,1,0:T(8,128)} %pad_maximum_fusion) | data formatting | bytes 2534400 | tf_op jit(solution)/shard_map/reshape | solution.py:60
  190.2 13.8 %copy.96 = f32[6,52800]{0,1:T(8,128)} copy(f32[6,52800]{1,0:T(8,128)S(1)} %reshape.217) | data formatting | bytes 2534400 | tf_op jit(solution)/shard_map/reshape | solution.py:60
  204.0 67.8 %gather_fusion.12 = f32[32000,6]{1,0:T(8,128)} fusion(f32[6,52800]{0,1:T(8,128)} %copy.96, s32[32768]{0:T(1024)S(1)} %pad_clamp_fusion), kind=kCustom, calls=%fused_computation.12 | custom fusion | bytes 1664000 | tf_op jit(solution)/shard_map/jit(_take)/gather | solution.py:68
  271.8 10.0 %copy.97 = f32[125,256,6]{0,2,1:T(8,128)S(1)} copy(f32[125,256,6]{2,1,0:T(8,128)} %bitcast.208) | data formatting | bytes 1536000 | tf_op jit(solution)/shard_map/jit(_take)/gather | solution.py:68
  283.2 5.1 %all-to-all-start.1 = ((f32[750,16,16]{0,2,1:T(8,128)}), f32[750,16,16]{0,2,1:T(8,128)S(1)}, u32[]{:S(2)}, u32[]{:S(2)}) async-start(f32[750,16,16]{0,2,1:T(8,128)} %select_n.180), calls=%async_computation.1 | async-start | bytes 1572864 | tf_op jit(solution)/shard_map/all_to_all | solution.py:132
  289.8 19.7 %all-to-all-done.1 = f32[750,16,16]{0,2,1:T(8,128)S(1)} async-done(((f32[750,16,16]{0,2,1:T(8,128)}), f32[750,16,16]{0,2,1:T(8,128)S(1)}, u32[]{:S(2)}, u32[]{:S(2)}) %all-to-all-start.1) | async-done | bytes 768032 | tf_op jit(solution)/shard_map/all_to_all | solution.py:132
  309.5 4.9 %copy.98 = f32[750,16,16]{2,1,0:T(8,128)} copy(f32[750,16,16]{0,2,1:T(8,128)S(1)} %all-to-all-done.1) | data formatting | bytes 1536000 | tf_op jit(solution)/shard_map/all_to_all | solution.py:132
  314.4 4.9 %reshape.218 = f32[6,5,5,5,256]{4,3,2,1,0:T(8,128)S(1)} reshape(f32[750,16,16]{2,1,0:T(8,128)} %copy.98) | data formatting | bytes 1536000 | tf_op jit(solution)/shard_map/reshape | solution.py:139
  (193 shorter events, 60.6 us)
Async XLA Ops:
  0.6 9.3 %copy-start.18 = (s32[4]{0:T(128)S(1)}, s32[4]{0:T(128)}, u32[]{:S(2)}) copy-start(s32[4]{0:T(128)} %constant.221) | copy-start | bytes 52
  0.6 9.3 %copy-start.19 = (s32[4]{0:T(128)S(1)}, s32[4]{0:T(128)}, u32[]{:S(2)}) copy-start(s32[4]{0:T(128)} %constant.222) | copy-start | bytes 52
  0.7 9.3 %copy-start.2 = (f32[6,16,16,128]{3,2,1,0:T(8,128)S(1)}, f32[6,16,16,128]{3,2,1,0:T(8,128)}, u32[]{:S(2)}) copy-start(f32[6,16,16,128]{3,2,1,0:T(8,128)} %param.17) | copy-start | bytes 2359300
  3.2 18.3 %copy-start.17 = (s32[128]{0:T(128)}, s32[128]{0:T(128)S(1)}, u32[]{:S(2)}) copy-start(s32[128]{0:T(128)S(1)} %fusion.239) | copy-start | bytes 1540
  6.2 36.8 %collective-permute-start = (f32[4,16,2,128]{3,2,1,0:T(2,128)S(1)}, f32[4,16,2,128]{3,2,1,0:T(2,128)S(1)}, u32[]{:S(2)}, u32[]{:S(2)}) collective-permute-start(f32[4,16,2,128]{3,2,1,0:T(2,128)S(1)} %get-tuple-element.86), channel_id=1, source_target_pairs={{0,4},{4,8},{8,12},{1,5},{5,9},{9,13},{2,6},{6,10},{10,14},{3,7},{... | collective-permute-start | bytes 196616 | tf_op jit(solution)/shard_map/ppermute | solution.py:17
  8.6 34.4 %collective-permute-start.1 = (f32[4,16,2,128]{3,2,1,0:T(2,128)S(1)}, f32[4,16,2,128]{3,2,1,0:T(2,128)S(1)}, u32[]{:S(2)}, u32[]{:S(2)}) collective-permute-start(f32[4,16,2,128]{3,2,1,0:T(2,128)S(1)} %get-tuple-element.87), channel_id=1, source_target_pairs={{4,0},{8,4},{12,8},{5,1},{9,5},{13,9},{6,2},{10,6},{14,10},{7,3},{... | collective-permute-start | bytes 196616 | tf_op jit(solution)/shard_map/ppermute | solution.py:19
  9.9 7.4 %copy-start.13 = (s32[1024]{0:T(1024)}, s32[1024]{0:T(1024)S(1)}, u32[]{:S(2)}) copy-start(s32[1024]{0:T(1024)S(1)} %get-tuple-element.120) | copy-start | bytes 12292
  10.5 10.8 %copy-start.16 = (s32[128,3]{0,1:T(4,128)S(1)}, s32[128,3]{0,1:T(4,128)}, u32[]{:S(2)}) copy-start(s32[128,3]{0,1:T(4,128)} %param.20) | copy-start | bytes 4612
  11.7 28.4 %collective-permute-start.4 = (f32[4,16,16,2]{3,2,1,0:T(8,128)}, f32[4,16,16,2]{3,2,1,0:T(8,128)S(1)}, u32[]{:S(2)}, u32[]{:S(2)}) collective-permute-start(f32[4,16,16,2]{3,2,1,0:T(8,128)} %get-tuple-element.88), channel_id=1, source_target_pairs={{0,1},{1,2},{2,3},{4,5},{5,6},{6,7},{8,9},{9,10},{10,11},{12,13},{... | collective-permute-start | bytes 24584 | tf_op jit(solution)/shard_map/ppermute | solution.py:17
  16.0 25.3 %collective-permute-start.5 = (f32[4,16,16,2]{3,2,1,0:T(8,128)}, f32[4,16,16,2]{3,2,1,0:T(8,128)}, u32[]{:S(2)}, u32[]{:S(2)}) collective-permute-start(f32[4,16,16,2]{3,2,1,0:T(8,128)} %get-tuple-element.89), channel_id=1, source_target_pairs={{1,0},{2,1},{3,2},{5,4},{6,5},{7,6},{9,8},{10,9},{11,10},{13,12},{... | collective-permute-start | bytes 24584 | tf_op jit(solution)/shard_map/ppermute | solution.py:19
  17.9 25.2 %collective-permute-start.2 = (f32[4,2,16,128]{3,2,1,0:T(8,128)S(1)}, f32[4,2,16,128]{3,2,1,0:T(8,128)S(1)}, u32[]{:S(2)}, u32[]{:S(2)}) collective-permute-start(f32[4,2,16,128]{3,2,1,0:T(8,128)S(1)} %get-tuple-element.91), channel_id=1, source_target_pairs={{0,16},{1,17},{2,18},{3,19},{4,20},{5,21},{6,22},{7,23},{8,24},{9,... | collective-permute-start | bytes 196616 | tf_op jit(solution)/shard_map/ppermute | solution.py:17
  23.1 16.8 %all-to-all-start = ((s32[3,16,16]{2,0,1:T(4,128)}), s32[3,16,16]{2,0,1:T(4,128)S(1)}, u32[]{:S(2)}, u32[]{:S(2)}) async-start(s32[3,16,16]{2,0,1:T(4,128)} %copy.91), calls=%async_computation | async-start | bytes 65536 | tf_op jit(solution)/shard_map/all_to_all | solution.py:127
  40.0 6.2 %collective-permute-start.3 = (f32[4,2,16,128]{3,2,1,0:T(8,128)S(1)}, f32[4,2,16,128]{3,2,1,0:T(8,128)S(1)}, u32[]{:S(2)}, u32[]{:S(2)}) collective-permute-start(f32[4,2,16,128]{3,2,1,0:T(8,128)S(1)} %get-tuple-element.90), channel_id=1, source_target_pairs={{16,0},{17,1},{18,2},{19,3},{20,4},{21,5},{22,6},{23,7},{24,8},{25... | collective-permute-start | bytes 196616 | tf_op jit(solution)/shard_map/ppermute | solution.py:19
  52.8 7.7 %copy-start.11 = (f32[4,16,16,128]{3,2,1,0:T(8,128)S(1)}, f32[4,16,16,128]{3,2,1,0:T(8,128)}, u32[]{:S(2)}) copy-start(f32[4,16,16,128]{3,2,1,0:T(8,128)} %gather_fusion.3) | copy-start | bytes 1572868
  53.8 21.1 %collective-permute-start.8 = (f32[4,2,16,128]{3,2,1,0:T(8,128)S(1)}, f32[4,2,16,128]{3,2,1,0:T(8,128)S(1)}, u32[]{:S(2)}, u32[]{:S(2)}) collective-permute-start(f32[4,2,16,128]{3,2,1,0:T(8,128)S(1)} %get-tuple-element.85), channel_id=1, source_target_pairs={{0,16},{1,17},{2,18},{3,19},{4,20},{5,21},{6,22},{7,23},{8,24},{9,... | collective-permute-start | bytes 196616 | tf_op jit(solution)/shard_map/ppermute | solution.py:17
  55.4 20.5 %collective-permute-start.9 = (f32[4,2,16,128]{3,2,1,0:T(8,128)S(1)}, f32[4,2,16,128]{3,2,1,0:T(8,128)S(1)}, u32[]{:S(2)}, u32[]{:S(2)}) collective-permute-start(f32[4,2,16,128]{3,2,1,0:T(8,128)S(1)} %get-tuple-element.84), channel_id=1, source_target_pairs={{16,0},{17,1},{18,2},{19,3},{20,4},{21,5},{22,6},{23,7},{24,8},{25... | collective-permute-start | bytes 196616 | tf_op jit(solution)/shard_map/ppermute | solution.py:19
  56.9 13.2 %collective-permute-start.10 = (f32[4,16,16,2]{3,2,1,0:T(8,128)S(1)}, f32[4,16,16,2]{3,2,1,0:T(8,128)S(1)}, u32[]{:S(2)}, u32[]{:S(2)}) collective-permute-start(f32[4,16,16,2]{3,2,1,0:T(8,128)S(1)} %get-tuple-element.82), channel_id=1, source_target_pairs={{0,1},{1,2},{2,3},{4,5},{5,6},{6,7},{8,9},{9,10},{10,11},{12,13},{... | collective-permute-start | bytes 24584 | tf_op jit(solution)/shard_map/ppermute | solution.py:17
  59.3 15.0 %collective-permute-start.11 = (f32[4,16,16,2]{3,2,1,0:T(8,128)S(1)}, f32[4,16,16,2]{3,2,1,0:T(8,128)S(1)}, u32[]{:S(2)}, u32[]{:S(2)}) collective-permute-start(f32[4,16,16,2]{3,2,1,0:T(8,128)S(1)} %get-tuple-element.83), channel_id=1, source_target_pairs={{1,0},{2,1},{3,2},{5,4},{6,5},{7,6},{9,8},{10,9},{11,10},{13,12},{... | collective-permute-start | bytes 24584 | tf_op jit(solution)/shard_map/ppermute | solution.py:19
  60.6 15.3 %collective-permute-start.6 = (f32[4,16,2,128]{3,2,1,0:T(2,128)S(1)}, f32[4,16,2,128]{3,2,1,0:T(2,128)S(1)}, u32[]{:S(2)}, u32[]{:S(2)}) collective-permute-start(f32[4,16,2,128]{3,2,1,0:T(2,128)S(1)} %get-tuple-element.80), channel_id=1, source_target_pairs={{0,4},{4,8},{8,12},{1,5},{5,9},{9,13},{2,6},{6,10},{10,14},{3,7},{... | collective-permute-start | bytes 196616 | tf_op jit(solution)/shard_map/ppermute | solution.py:17
  70.1 5.8 %collective-permute-start.7 = (f32[4,16,2,128]{3,2,1,0:T(2,128)S(1)}, f32[4,16,2,128]{3,2,1,0:T(2,128)S(1)}, u32[]{:S(2)}, u32[]{:S(2)}) collective-permute-start(f32[4,16,2,128]{3,2,1,0:T(2,128)S(1)} %get-tuple-element.81), channel_id=1, source_target_pairs={{4,0},{8,4},{12,8},{5,1},{9,5},{13,9},{6,2},{10,6},{14,10},{7,3},{... | collective-permute-start | bytes 196616 | tf_op jit(solution)/shard_map/ppermute | solution.py:19
  74.7 1.0 copy-start.8
  83.5 10.6 %copy-start.12 = (f32[4,16,16,128]{3,2,1,0:T(8,128)S(1)}, f32[4,16,16,128]{3,2,1,0:T(8,128)}, u32[]{:S(2)}) copy-start(f32[4,16,16,128]{3,2,1,0:T(8,128)} %gather_fusion.6) | copy-start | bytes 1572868
  84.4 24.7 %collective-permute-start.14 = (f32[4,2,16,128]{3,2,1,0:T(8,128)S(1)}, f32[4,2,16,128]{3,2,1,0:T(8,128)S(1)}, u32[]{:S(2)}, u32[]{:S(2)}) collective-permute-start(f32[4,2,16,128]{3,2,1,0:T(8,128)S(1)} %get-tuple-element.79), channel_id=1, source_target_pairs={{0,16},{1,17},{2,18},{3,19},{4,20},{5,21},{6,22},{7,23},{8,24},{9,... | collective-permute-start | bytes 196616 | tf_op jit(solution)/shard_map/ppermute | solution.py:17
  88.7 21.4 %collective-permute-start.15 = (f32[4,2,16,128]{3,2,1,0:T(8,128)S(1)}, f32[4,2,16,128]{3,2,1,0:T(8,128)S(1)}, u32[]{:S(2)}, u32[]{:S(2)}) collective-permute-start(f32[4,2,16,128]{3,2,1,0:T(8,128)S(1)} %get-tuple-element.78), channel_id=1, source_target_pairs={{16,0},{17,1},{18,2},{19,3},{20,4},{21,5},{22,6},{23,7},{24,8},{25... | collective-permute-start | bytes 196616 | tf_op jit(solution)/shard_map/ppermute | solution.py:19
  90.2 14.2 %collective-permute-start.16 = (f32[4,16,16,2]{3,2,1,0:T(8,128)S(1)}, f32[4,16,16,2]{3,2,1,0:T(8,128)S(1)}, u32[]{:S(2)}, u32[]{:S(2)}) collective-permute-start(f32[4,16,16,2]{3,2,1,0:T(8,128)S(1)} %get-tuple-element.76), channel_id=1, source_target_pairs={{0,1},{1,2},{2,3},{4,5},{5,6},{6,7},{8,9},{9,10},{10,11},{12,13},{... | collective-permute-start | bytes 24584 | tf_op jit(solution)/shard_map/ppermute | solution.py:17
  92.8 15.7 %collective-permute-start.17 = (f32[4,16,16,2]{3,2,1,0:T(8,128)S(1)}, f32[4,16,16,2]{3,2,1,0:T(8,128)S(1)}, u32[]{:S(2)}, u32[]{:S(2)}) collective-permute-start(f32[4,16,16,2]{3,2,1,0:T(8,128)S(1)} %get-tuple-element.77), channel_id=1, source_target_pairs={{1,0},{2,1},{3,2},{5,4},{6,5},{7,6},{9,8},{10,9},{11,10},{13,12},{... | collective-permute-start | bytes 24584 | tf_op jit(solution)/shard_map/ppermute | solution.py:19
  94.2 16.0 %collective-permute-start.12 = (f32[4,16,2,128]{3,2,1,0:T(2,128)S(1)}, f32[4,16,2,128]{3,2,1,0:T(2,128)S(1)}, u32[]{:S(2)}, u32[]{:S(2)}) collective-permute-start(f32[4,16,2,128]{3,2,1,0:T(2,128)S(1)} %get-tuple-element.74), channel_id=1, source_target_pairs={{0,4},{4,8},{8,12},{1,5},{5,9},{9,13},{2,6},{6,10},{10,14},{3,7},{... | collective-permute-start | bytes 196616 | tf_op jit(solution)/shard_map/ppermute | solution.py:17
  104.4 5.8 %collective-permute-start.13 = (f32[4,16,2,128]{3,2,1,0:T(2,128)S(1)}, f32[4,16,2,128]{3,2,1,0:T(2,128)S(1)}, u32[]{:S(2)}, u32[]{:S(2)}) collective-permute-start(f32[4,16,2,128]{3,2,1,0:T(2,128)S(1)} %get-tuple-element.75), channel_id=1, source_target_pairs={{4,0},{8,4},{12,8},{5,1},{9,5},{13,9},{6,2},{10,6},{14,10},{7,3},{... | collective-permute-start | bytes 196616 | tf_op jit(solution)/shard_map/ppermute | solution.py:19
  109.0 1.0 copy-start.9
  117.8 10.6 %copy-start.10 = (f32[4,16,16,128]{3,2,1,0:T(8,128)S(1)}, f32[4,16,16,128]{3,2,1,0:T(8,128)}, u32[]{:S(2)}) copy-start(f32[4,16,16,128]{3,2,1,0:T(8,128)} %gather_fusion.9) | copy-start | bytes 1572868
  118.8 24.8 %collective-permute-start.20 = (f32[4,2,16,128]{3,2,1,0:T(8,128)S(1)}, f32[4,2,16,128]{3,2,1,0:T(8,128)S(1)}, u32[]{:S(2)}, u32[]{:S(2)}) collective-permute-start(f32[4,2,16,128]{3,2,1,0:T(8,128)S(1)} %get-tuple-element.73), channel_id=1, source_target_pairs={{0,16},{1,17},{2,18},{3,19},{4,20},{5,21},{6,22},{7,23},{8,24},{9,... | collective-permute-start | bytes 196616 | tf_op jit(solution)/shard_map/ppermute | solution.py:17
  123.1 21.6 %collective-permute-start.21 = (f32[4,2,16,128]{3,2,1,0:T(8,128)S(1)}, f32[4,2,16,128]{3,2,1,0:T(8,128)S(1)}, u32[]{:S(2)}, u32[]{:S(2)}) collective-permute-start(f32[4,2,16,128]{3,2,1,0:T(8,128)S(1)} %get-tuple-element.72), channel_id=1, source_target_pairs={{16,0},{17,1},{18,2},{19,3},{20,4},{21,5},{22,6},{23,7},{24,8},{25... | collective-permute-start | bytes 196616 | tf_op jit(solution)/shard_map/ppermute | solution.py:19
  124.6 14.4 %collective-permute-start.22 = (f32[4,16,16,2]{3,2,1,0:T(8,128)S(1)}, f32[4,16,16,2]{3,2,1,0:T(8,128)S(1)}, u32[]{:S(2)}, u32[]{:S(2)}) collective-permute-start(f32[4,16,16,2]{3,2,1,0:T(8,128)S(1)} %get-tuple-element.70), channel_id=1, source_target_pairs={{0,1},{1,2},{2,3},{4,5},{5,6},{6,7},{8,9},{9,10},{10,11},{12,13},{... | collective-permute-start | bytes 24584 | tf_op jit(solution)/shard_map/ppermute | solution.py:17
  127.1 15.9 %collective-permute-start.23 = (f32[4,16,16,2]{3,2,1,0:T(8,128)S(1)}, f32[4,16,16,2]{3,2,1,0:T(8,128)S(1)}, u32[]{:S(2)}, u32[]{:S(2)}) collective-permute-start(f32[4,16,16,2]{3,2,1,0:T(8,128)S(1)} %get-tuple-element.71), channel_id=1, source_target_pairs={{1,0},{2,1},{3,2},{5,4},{6,5},{7,6},{9,8},{10,9},{11,10},{13,12},{... | collective-permute-start | bytes 24584 | tf_op jit(solution)/shard_map/ppermute | solution.py:19
  128.5 16.2 %collective-permute-start.18 = (f32[4,16,2,128]{3,2,1,0:T(2,128)S(1)}, f32[4,16,2,128]{3,2,1,0:T(2,128)S(1)}, u32[]{:S(2)}, u32[]{:S(2)}) collective-permute-start(f32[4,16,2,128]{3,2,1,0:T(2,128)S(1)} %get-tuple-element.68), channel_id=1, source_target_pairs={{0,4},{4,8},{8,12},{1,5},{5,9},{9,13},{2,6},{6,10},{10,14},{3,7},{... | collective-permute-start | bytes 196616 | tf_op jit(solution)/shard_map/ppermute | solution.py:17
  138.9 5.8 %collective-permute-start.19 = (f32[4,16,2,128]{3,2,1,0:T(2,128)S(1)}, f32[4,16,2,128]{3,2,1,0:T(2,128)S(1)}, u32[]{:S(2)}, u32[]{:S(2)}) collective-permute-start(f32[4,16,2,128]{3,2,1,0:T(2,128)S(1)} %get-tuple-element.69), channel_id=1, source_target_pairs={{4,0},{8,4},{12,8},{5,1},{9,5},{13,9},{6,2},{10,6},{14,10},{7,3},{... | collective-permute-start | bytes 196616 | tf_op jit(solution)/shard_map/ppermute | solution.py:19
  147.2 1.1 copy-start.4
  147.2 1.4 copy-start.6
  148.6 5.9 %copy-start.15 = (s32[125]{0:T(128)S(1)}, s32[125]{0:T(128)}, u32[]{:S(2)}) copy-start(s32[125]{0:T(128)} %add.487) | copy-start | bytes 1504
  148.9 33.3 %copy-start.1 = (f32[6,16,16,128]{3,2,1,0:T(8,128)}, f32[6,16,16,128]{3,2,1,0:T(8,128)S(1)}, u32[]{:S(2)}) copy-start(f32[6,16,16,128]{3,2,1,0:T(8,128)S(1)} %multiply_add_fusion) | copy-start | bytes 2359300
  148.9 6.5 %collective-permute-start.24 = (f32[6,2,16,128]{3,2,1,0:T(8,128)S(1)}, f32[6,2,16,128]{3,2,1,0:T(8,128)S(1)}, u32[]{:S(2)}, u32[]{:S(2)}) collective-permute-start(f32[6,2,16,128]{3,2,1,0:T(8,128)S(1)} %get-tuple-element.34), channel_id=1, source_target_pairs={{0,16},{1,17},{2,18},{3,19},{4,20},{5,21},{6,22},{7,23},{8,24},{9,... | collective-permute-start | bytes 294920 | tf_op jit(solution)/shard_map/ppermute | solution.py:17
  153.2 6.5 %collective-permute-start.25 = (f32[6,2,16,128]{3,2,1,0:T(8,128)S(1)}, f32[6,2,16,128]{3,2,1,0:T(8,128)S(1)}, u32[]{:S(2)}, u32[]{:S(2)}) collective-permute-start(f32[6,2,16,128]{3,2,1,0:T(8,128)S(1)} %get-tuple-element.35), channel_id=1, source_target_pairs={{16,0},{17,1},{18,2},{19,3},{20,4},{21,5},{22,6},{23,7},{24,8},{25... | collective-permute-start | bytes 294920 | tf_op jit(solution)/shard_map/ppermute | solution.py:19
  159.8 2.6 collective-permute-start.26
  161.1 3.2 %collective-permute-start.27 = (f32[6,20,2,128]{3,2,1,0:T(2,128)S(1)}, f32[6,20,2,128]{3,2,1,0:T(2,128)S(1)}, u32[]{:S(2)}, u32[]{:S(2)}) collective-permute-start(f32[6,20,2,128]{3,2,1,0:T(2,128)S(1)} %get-tuple-element.33), channel_id=1, source_target_pairs={{4,0},{8,4},{12,8},{5,1},{9,5},{13,9},{6,2},{10,6},{14,10},{7,3},{... | collective-permute-start | bytes 368648 | tf_op jit(solution)/shard_map/ppermute | solution.py:19
  168.5 6.4 %collective-permute-start.28 = (f32[6,20,20,2]{2,1,3,0:T(8,128)S(1)}, f32[6,20,20,2]{2,1,3,0:T(8,128)S(1)}, u32[]{:S(2)}, u32[]{:S(2)}) collective-permute-start(f32[6,20,20,2]{2,1,3,0:T(8,128)S(1)} %copy.92), channel_id=1, source_target_pairs={{0,1},{1,2},{2,3},{4,5},{5,6},{6,7},{8,9},{9,10},{10,11},{12,13},{... | collective-permute-start | bytes 57608 | tf_op jit(solution)/shard_map/ppermute | solution.py:17
  173.2 7.0 %collective-permute-start.29 = (f32[6,20,20,2]{2,1,3,0:T(8,128)S(1)}, f32[6,20,20,2]{2,1,3,0:T(8,128)S(1)}, u32[]{:S(2)}, u32[]{:S(2)}) collective-permute-start(f32[6,20,20,2]{2,1,3,0:T(8,128)S(1)} %copy.93), channel_id=1, source_target_pairs={{1,0},{2,1},{3,2},{5,4},{6,5},{7,6},{9,8},{10,9},{11,10},{13,12},{... | collective-permute-start | bytes 57608 | tf_op jit(solution)/shard_map/ppermute | solution.py:19
  282.0 6.3 %copy-start.14 = (f32[128,15]{0,1:T(8,128)S(1)}, f32[128,15]{0,1:T(8,128)}, u32[]{:S(2)}) copy-start(f32[128,15]{0,1:T(8,128)} %param.21) | copy-start | bytes 23044
  283.2 26.3 %all-to-all-start.1 = ((f32[750,16,16]{0,2,1:T(8,128)}), f32[750,16,16]{0,2,1:T(8,128)S(1)}, u32[]{:S(2)}, u32[]{:S(2)}) async-start(f32[750,16,16]{0,2,1:T(8,128)} %select_n.180), calls=%async_computation.1 | async-start | bytes 1572864 | tf_op jit(solution)/shard_map/all_to_all | solution.py:132
  (4 other events, 3.9 us)
where the time goes:
time: 323 us; the launch traced here: 321 us
  local copies, waits for them, and re-layouts  143 us (44%)
  starting transfers between devices  77.6 us (24%)
  waiting for transfers between devices  73.1 us (23%)
  other arithmetic  25.4 us (8%)
    gather x2, local copies, waits for them, and re-layouts, gather_tiles(): picked = jnp.take(flat_grid, offsets[:, None] + starts[None, :], axis=1)  77.8 us
    ppermute x15, starting transfers between devices, padded_2(): lax.ppermute(tail, axis, [(i, (i + 1) % count) for i in range(ends)])  42.4 us
    ppermute x15, waiting for transfers between devices, padded_2(): lax.ppermute(tail, axis, [(i, (i + 1) % count) for i in range(ends)])  25.6 us
    ppermute x15, waiting for transfers between devices, padded_2(): lax.ppermute(head, axis, [((i + 1) % count, i) for i in range(ends)])  22.1 us
    ppermute x15, starting transfers between devices, padded_2(): lax.ppermute(head, axis, [((i + 1) % count, i) for i in range(ends)])  19.7 us
    all_to_all x1, waiting for transfers between devices, local(): lax.all_to_all(donor_tiles.reshape(750, group_size, slot_count), ('gy', '...  19.7 us
    reshape x2, local copies, waits for them, and re-layouts, gather_tiles(): flat_grid = donor_grid.reshape(components, extent_x * extent_y * extent_z)  17.2 us
    all_to_all x1, starting transfers between devices, local(): lax.all_to_all(corner_send, ('gy', 'gz'), split_axis=1, concat_axis=1, ti...  10.3 us
  transfers between devices with their start and end apart: 32, of which 14 were waited for; matrix products, arithmetic and copies ran while one was open for 4% of the time, Pallas kernels for 0%

commit v1 on v0

v1 whole, which is shorter than its diff:
```python
import functools

import jax
import jax.numpy as jnp
from jax import lax
from jax.experimental import pallas as pl
from jax.experimental.pallas import tpu as pltpu
from jax.sharding import PartitionSpec as P

step_size = 0.25
MESH = pl.DeviceIdType.MESH
Y_COMPS = (0, 2, 3, 5)
Z_COMPS = (0, 1, 3, 4)
F32 = jnp.float32
HI = lax.Precision.HIGHEST


def dot(a, b, dims=((1,), (0,))):
    return lax.dot_general(a, b, (dims, ((), ())), precision=HI, preferred_element_type=F32)


def kernel(
    sizes, fields, eps, owner, data, out, recept,
    T, F, H, inv, ys, yr, zs, zr, yfs, yfr, zfs, zfr,
    req, reqr, ans, ansr, W, wz_in, wz_halo, perm,
    load_sem, send, recv, fsend, frecv, rsend, rrecv, asend, arecv,
):
    nx, ny, nz, cap = sizes
    group = ny * nz
    cx, cy, cz = eps.shape
    x, y, z = lax.axis_index("gx"), lax.axis_index("gy"), lax.axis_index("gz")
    me = y * nz + z
    y0, y1 = 8, 8 + cy

    loads = [
        pltpu.make_async_copy(fields, T.at[0, :, pl.ds(2, cx), pl.ds(8, cy), :], load_sem.at[0]),
        pltpu.make_async_copy(fields, F.at[:, pl.ds(2, cx), pl.ds(8, cy), :], load_sem.at[1]),
        pltpu.make_async_copy(eps, inv, load_sem.at[2]),
    ]
    for copy in loads:
        copy.start()

    def clear(ref):
        ref[...] = jnp.zeros(ref.shape, F32)

    for m in range(4):
        for lo in (0, cx + 2):
            clear(T.at[m, :, pl.ds(lo, 2)])
    for lo in (0, cx + 2):
        clear(F.at[:, pl.ds(lo, 2)])
        clear(H.at[pl.ds(lo, 2)])
    for lo in (0, y1):
        clear(F.at[:, pl.ds(2, cx), pl.ds(lo, 8)])
        clear(H.at[pl.ds(2, cx), pl.ds(lo, 8)])
    for ref in (yr, zr, yfr, zfr):
        clear(ref)

    barrier = pltpu.get_barrier_semaphore()
    others = []
    for d in range(1, group):
        t = lax.rem(me + d, group)
        others.append((x, t // nz, lax.rem(t, nz)))
    for target in others:
        pl.semaphore_signal(barrier, inc=1, device_id=target, device_id_type=MESH)

    has = {"xl": x > 0, "xh": x < nx - 1, "yl": y > 0, "yh": y < ny - 1, "zl": z > 0, "zh": z < nz - 1}
    dev = {
        "xl": (x - 1, y, z), "xh": (x + 1, y, z), "yl": (x, y - 1, z), "yh": (x, y + 1, z),
        "zl": (x, y, z - 1), "zh": (x, y, z + 1),
    }
    for side in ("xl", "xh"):
        @pl.when(has[side])
        def _():
            pl.semaphore_signal(barrier, inc=1, device_id=dev[side], device_id_type=MESH)

    rows = owner.shape[0]
    col = lax.broadcasted_iota(jnp.int32, (rows, 128), 1)
    row = lax.broadcasted_iota(jnp.int32, (rows, 128), 0)
    own = owner[...]
    hits = (own == col).astype(F32)
    earlier = dot((lax.broadcasted_iota(jnp.int32, (rows, rows), 1)
                   < lax.broadcasted_iota(jnp.int32, (rows, rows), 0)).astype(F32), hits)
    slot = jnp.sum(earlier * hits, axis=1, keepdims=True).astype(jnp.int32)
    flat = own * cap + slot
    slots = group * cap
    perm[...] = (flat == lax.broadcasted_iota(jnp.int32, (rows, slots), 1)).astype(F32)
    packed = dot(perm[...], data[...], ((0,), (0,)))
    for o in range(group):
        req[o] = packed[o * cap:(o + 1) * cap]
    reqr[me] = req[me]

    for copy in loads:
        copy.wait()
    inv[...] = 1.0 / (12.0 * inv[...])

    pl.semaphore_wait(barrier, group - 1 + has["xl"].astype(jnp.int32) + has["xh"].astype(jnp.int32))

    def remote(src, dst, s, r, target):
        return pltpu.make_async_remote_copy(
            src_ref=src, dst_ref=dst, send_sem=s, recv_sem=r, device_id=target, device_id_type=MESH)

    def request(d):
        return remote(req.at[(me + d) % group], reqr.at[me], rsend.at[d], rrecv.at[d], others[d - 1])

    def answer(d):
        return remote(ans.at[(me + d) % group], ansr.at[me], asend.at[d], arecv.at[d], others[d - 1])

    lane = lax.broadcasted_iota(jnp.int32, (cy, cz), 1)
    opposite = {"xl": "xh", "xh": "xl", "yl": "yh", "yh": "yl", "zl": "zh", "zh": "zl"}

    def x_copies(m, side):
        lo_src, lo_dst = (2, cx + 2) if side == "xl" else (cx, 0)
        base = 0 if side == "xl" else 2
        return [
            remote(T.at[m, pl.ds(c, 2), pl.ds(lo_src, 2), pl.ds(8, cy)],
                   T.at[m, pl.ds(c, 2), pl.ds(lo_dst, 2), pl.ds(8, cy)],
                   send.at[m, base + i], recv.at[m, base + i], dev[side])
            for i, c in enumerate((1, 4))
        ]

    def y_copies(m, side):
        k = 0 if side == "yl" else 1
        return [remote(ys.at[m, k], yr.at[m, k], send.at[m, 4 + k], recv.at[m, 4 + k], dev[side])]

    def z_copies(m, side):
        k = 0 if side == "zl" else 1
        return [remote(zs.at[m], zr.at[m, k], send.at[m, 6 + k], recv.at[m, 6 + k], dev[side])]

    def start(copies, side):
        @pl.when(has[side])
        def _():
            for copy in copies:
                copy.start()

    def finish_recv(copies, side):
        @pl.when(has[opposite[side]])
        def _():
            for copy in copies:
                copy.wait_recv()

    def finish_send(copies, side):
        @pl.when(has[side])
        def _():
            for copy in copies:
                copy.wait_send()

    def shifts_z(f, edge):
        lo2 = pltpu.roll(jnp.where(lane >= cz - 2, edge, f), 2, 1)
        lo1 = pltpu.roll(jnp.where(lane >= cz - 1, edge, f), 1, 1)
        hi2 = pltpu.roll(jnp.where(lane < 2, edge, f), cz - 2, 1)
        hi1 = pltpu.roll(jnp.where(lane < 1, edge, f), cz - 1, 1)
        return (lo2 - hi2) + 8.0 * (hi1 - lo1)

    per = cz // 16

    def step(m, carry):
        for side in ("xl", "xh"):
            start(x_copies(m, side), side)

        def pack(g, c_):
            strip = jnp.zeros((cy, cz), F32)
            for i in range(per):
                px = 2 + g * per + i
                for q, c in enumerate(Z_COMPS):
                    b = (i * 4 + q) * 4
                    strip = jnp.where(lane // 4 == i * 4 + q,
                                      pltpu.roll(T[m, c, px, y0:y1, :], (b + 2) % cz, 1), strip)
            zs[m, g] = strip
            return c_

        lax.fori_loop(0, cx // per, pack, 0)
        for side in ("zl", "zh"):
            start(z_copies(m, side), side)
        for q, c in enumerate(Y_COMPS):
            ys[m, 0, :, 2 * q:2 * q + 2, :] = T[m, c, 2:2 + cx, y0:y0 + 2, :]
            ys[m, 1, :, 2 * q:2 * q + 2, :] = T[m, c, 2:2 + cx, y1 - 2:y1, :]
        for side in ("yl", "yh"):
            start(y_copies(m, side), side)

        @pl.when(m == 0)
        def _():
            for d in range(1, group):
                request(d).start()

        for side in ("zl", "zh"):
            finish_recv(z_copies(m, side), side)
        for side in ("yl", "yh"):
            finish_recv(y_copies(m, side), side)
        for side in ("xl", "xh"):
            finish_recv(x_copies(m, side), side)
        for q, c in enumerate(Y_COMPS):
            T[m, c, 2:2 + cx, y0 - 2:y0, :] = yr[m, 1, :, 2 * q:2 * q + 2, :]
            T[m, c, 2:2 + cx, y1:y1 + 2, :] = yr[m, 0, :, 2 * q:2 * q + 2, :]
        scale = step_size / (m + 1).astype(F32)

        def planes(g, c_):
            merged = jnp.where(lane % 4 < 2, zr[m, 1, g], zr[m, 0, g])
            for i in range(per):
                px = 2 + g * per + i

                def d_x(c):
                    at = lambda o: T[m, c, px + o, y0:y1, :]
                    return (at(-2) - at(2)) + 8.0 * (at(1) - at(-1))

                def d_y(c):
                    at = lambda o: T[m, c, px, y0 + o:y1 + o, :]
                    return (at(-2) - at(2)) + 8.0 * (at(1) - at(-1))

                def d_z(c):
                    b = (i * 4 + Z_COMPS.index(c)) * 4
                    edge = pltpu.roll(merged, (2 * cz - b - 2) % cz, 1)
                    return shifts_z(T[m, c, px, y0:y1, :], edge)

                se = inv[px - 2] * scale
                sh = scale / 12.0
                rates = (
                    (d_y(5) - d_z(4)) * se,
                    (d_z(3) - d_x(5)) * se,
                    (d_x(4) - d_y(3)) * se,
                    (d_z(1) - d_y(2)) * sh,
                    (d_x(2) - d_z(0)) * sh,
                    (d_y(0) - d_x(1)) * sh,
                )
                for c in range(6):
                    T[m + 1, c, px, y0:y1, :] = rates[c]
                    F[c, px, y0:y1, :] = F[c, px, y0:y1, :] + rates[c]
            return c_

        lax.fori_loop(0, cx // per, planes, 0)
        return carry

    lax.fori_loop(0, 4, step, 0)

    store = pltpu.make_async_copy(F.at[:, pl.ds(2, cx), pl.ds(8, cy), :], out, load_sem.at[3])
    store.start()

    def xf_copies(side):
        lo_src, lo_dst = (2, cx + 2) if side == "xl" else (cx, 0)
        base = 0 if side == "xl" else 1
        return [remote(F.at[:, pl.ds(lo_src, 2), pl.ds(8, cy)], F.at[:, pl.ds(lo_dst, 2), pl.ds(8, cy)],
                       fsend.at[base], frecv.at[base], dev[side])]

    def xh_copies(side):
        lo_src, lo_dst = (2, cx + 2) if side == "xl" else (cx, 0)
        base = 2 if side == "xl" else 3
        return [remote(H.at[pl.ds(lo_src, 2), pl.ds(8, cy)], H.at[pl.ds(lo_dst, 2), pl.ds(8, cy)],
                       fsend.at[base], frecv.at[base], dev[side])]

    def yf_copies(side):
        k = 0 if side == "yl" else 1
        return [remote(yfs.at[k], yfr.at[k], fsend.at[4 + k], frecv.at[4 + k], dev[side])]

    def zf_copies(side):
        k = 0 if side == "zl" else 1
        return [remote(zfs, zfr.at[k], fsend.at[6 + k], frecv.at[6 + k], dev[side])]

    for side in ("xl", "xh"):
        start(xf_copies(side), side)
    wide = cz // 32
    for g in range(cx // wide):
        strip = jnp.zeros((cy, cz), F32)
        for i in range(wide):
            for c in range(6):
                b = i * 32 + c * 4
                strip = jnp.where(lane // 4 == b // 4,
                                  pltpu.roll(F[c, 2 + g * wide + i, y0:y1, :], (b + 2) % cz, 1), strip)
        zfs[g] = strip
    for side in ("zl", "zh"):
        start(zf_copies(side), side)

    for d in range(1, group):
        request(d).wait_recv()
    if cap % 8 == 0:
        served = reqr[...].reshape(slots, 128)
    else:
        served = jnp.concatenate([reqr[o] for o in range(group)], axis=0)
    bx = served[:, 0:1].astype(jnp.int32)
    by = served[:, 1:2].astype(jnp.int32)
    bz = served[:, 2:3].astype(jnp.int32)

    def spread(offset, first):
        total = jnp.zeros(offset.shape, F32)
        for k in range(5):
            total = jnp.where(offset == k, served[:, first + k:first + k + 1], total)
        return total

    yrows = F.shape[2]
    for lo in range(0, W.shape[1], 128):
        li = lo + lax.broadcasted_iota(jnp.int32, (slots, 128), 1)
        W[:, lo:lo + 128] = spread(li // yrows - bx, 3) * spread(li % yrows - 6 - by, 8)
    li = lax.broadcasted_iota(jnp.int32, (slots, cz), 1)
    wz_in[...] = spread(li + 2 - bz, 13)
    tail = li % 4
    wz_halo[...] = jnp.where(li < 24, spread(jnp.where(tail < 2, tail, cz + tail) - bz, 13), 0.0)

    for side in ("zl", "zh"):
        finish_recv(zf_copies(side), side)
    for g in range(cx // wide):
        merged = jnp.where(lane % 4 < 2, zfr[1, g], zfr[0, g])
        for i in range(wide):
            H[2 + g * wide + i, y0:y1, :] = pltpu.roll(merged, (cz - i * 32) % cz, 1) if i else merged
    for side in ("xl", "xh"):
        start(xh_copies(side), side)
    for side in ("xl", "xh"):
        finish_recv(xf_copies(side), side)
        finish_recv(xh_copies(side), side)
    for k, lo in ((0, y0), (1, y1 - 2)):
        for c in range(6):
            yfs[k, :, 2 * c:2 * c + 2, :] = F[c, :, lo:lo + 2, :]
        yfs[k, :, 12:14, :] = H[:, lo:lo + 2, :]
    for side in ("yl", "yh"):
        start(yf_copies(side), side)
    for side in ("yl", "yh"):
        finish_recv(yf_copies(side), side)
    for k, lo in ((1, y0 - 2), (0, y1)):
        for c in range(6):
            F[c, :, lo:lo + 2, :] = yfr[k, :, 2 * c:2 * c + 2, :]
        H[:, lo:lo + 2, :] = yfr[k, :, 12:14, :]

    depth = W.shape[1]
    halo = dot(W[...], H[...].reshape(depth, cz)) * wz_halo[...]
    result = jnp.zeros((slots, cz), F32)
    for c in range(6):
        part = dot(W[...], F[c].reshape(depth, cz)) * wz_in[...]
        part = part + jnp.where(li // 4 == c, halo, 0.0)
        result = jnp.where(li == c, jnp.sum(part, axis=1, keepdims=True), result)
    for o in range(group):
        ans[o] = result[o * cap:(o + 1) * cap]
    for d in range(1, group):
        answer(d).start()
    ansr[me] = ans[me]
    for d in range(1, group):
        answer(d).wait_recv()
    if cap % 8 == 0:
        got = ansr[...].reshape(slots, 128)
    else:
        got = jnp.concatenate([ansr[o] for o in range(group)], axis=0)
    picked = dot(perm[...], got)
    recept[...] = jnp.transpose(picked)[0:8, :]

    store.wait()
    for m in range(4):
        for side in ("xl", "xh"):
            finish_send(x_copies(m, side), side)
        for side in ("yl", "yh"):
            finish_send(y_copies(m, side), side)
        for side in ("zl", "zh"):
            finish_send(z_copies(m, side), side)
    for side in ("xl", "xh"):
        finish_send(xf_copies(side), side)
        finish_send(xh_copies(side), side)
    for side in ("yl", "yh"):
        finish_send(yf_copies(side), side)
    for side in ("zl", "zh"):
        finish_send(zf_copies(side), side)
    for d in range(1, group):
        request(d).wait_send()
        answer(d).wait_send()


def local(sizes, fields, permittivity, donor_owner, donor_base, donor_weights):
    nx, ny, nz = sizes
    cx, cy, cz = permittivity.shape
    rows = donor_owner.shape[0]
    group = ny * nz
    cap = 2 * rows // group
    slots = group * cap
    data = jnp.concatenate([donor_base.astype(F32), donor_weights], axis=1)
    data = jnp.pad(data, ((0, 0), (0, 128 - data.shape[1])))
    vmem = pltpu.VMEM
    dma = pltpu.SemaphoreType.DMA
    yrows = cy + 16
    depth = (cx + 4) * yrows
    depth_pad = depth
    out, recept = pl.pallas_call(
        functools.partial(kernel, (nx, ny, nz, cap)),
        out_shape=(
            jax.ShapeDtypeStruct(fields.shape, F32),
            jax.ShapeDtypeStruct((8, rows), F32),
        ),
        in_specs=[
            pl.BlockSpec(memory_space=pl.ANY),
            pl.BlockSpec(memory_space=pl.ANY),
            pl.BlockSpec(memory_space=vmem),
            pl.BlockSpec(memory_space=vmem),
        ],
        out_specs=(pl.BlockSpec(memory_space=pl.ANY), pl.BlockSpec(memory_space=vmem)),
        scratch_shapes=[
            vmem((5, 6, cx + 4, yrows, cz), F32),
            vmem((6, cx + 4, yrows, cz), F32),
            vmem((cx + 4, yrows, cz), F32),
            vmem((cx, cy, cz), F32),
            vmem((4, 2, cx, 8, cz), F32),
            vmem((4, 2, cx, 8, cz), F32),
            vmem((4, cx * 16 // cz, cy, cz), F32),
            vmem((4, 2, cx * 16 // cz, cy, cz), F32),
            vmem((2, cx + 4, 16, cz), F32),
            vmem((2, cx + 4, 16, cz), F32),
            vmem((cx * 32 // cz, cy, cz), F32),
            vmem((2, cx * 32 // cz, cy, cz), F32),
            vmem((group, cap, 128), F32),
            vmem((group, cap, 128), F32),
            vmem((group, cap, 128), F32),
            vmem((group, cap, 128), F32),
            vmem((slots, depth_pad), F32),
            vmem((slots, cz), F32),
            vmem((slots, cz), F32),
            vmem((rows, slots), F32),
            dma((4,)),
            dma((4, 8)),
            dma((4, 8)),
            dma((8,)),
            dma((8,)),
            dma((group,)),
            dma((group,)),
            dma((group,)),
            dma((group,)),
        ],
        compiler_params=pltpu.CompilerParams(
            collective_id=0, has_side_effects=True, vmem_limit_bytes=40 * 1024 * 1024
        ),
    )(fields, permittivity, donor_owner, data)
    return out, recept[0:6]


def solution(mesh):
    sizes = (mesh.shape["gx"], mesh.shape["gy"], mesh.shape["gz"])
    placed = (
        P(None, "gx", "gy", "gz"),
        P("gx", "gy", "gz"),
        P(("gx", "gy", "gz"), None),
        P(("gx", "gy", "gz"), None),
        P(("gx", "gy", "gz"), None),
    )
    return jax.shard_map(
        functools.partial(local, sizes),
        mesh=mesh,
        in_specs=placed,
        out_specs=(P(None, "gx", "gy", "gz"), P(None, ("gx", "gy", "gz"))),
        check_vma=False,
    )
```

time: 323 us -> 60 us (0.19)
  local copies, waits for them, and re-layouts: 143 us -> 3.5 us
  starting transfers between devices: 77.6 us -> 0 us
  waiting for transfers between devices: 73.1 us -> 0 us
  Pallas kernels: 0 us -> 54.2 us
  other arithmetic: 25.4 us -> 1.39 us
    gather x15 -> x0, local copies, waits for them, and re-layouts: 91.9 us -> none  [the longest x2 77.8 us: gather_tiles(): picked = jnp.take(flat_grid, offsets[:, None] + starts[None, :], axis=1)]
    ppermute x30 -> x0, starting transfers between devices: 62.2 us -> none  [the longest x15 42.4 us: padded_2(): lax.ppermute(tail, axis, [(i, (i + 1) % count) for i in range(ends)])]
    pallas_call x0 -> x1, Pallas kernels: none -> 54.2 us  [local(): pl.pallas_call(functools.partial(kernel, (nx, ny, nz, cap)), out_shape=(j...]
    ppermute x30 -> x0, waiting for transfers between devices: 47.7 us -> none  [the longest x15 25.6 us: padded_2(): lax.ppermute(tail, axis, [(i, (i + 1) % count) for i in range(ends)])]
    all_to_all x2 -> x0, waiting for transfers between devices: 25.4 us -> none  [the longest x1 19.7 us: local(): lax.all_to_all(donor_tiles.reshape(750, group_size, slot_count), ('gy', '...]
    reshape x4 -> x0, local copies, waits for them, and re-layouts: 22.8 us -> none  [the longest x2 17.2 us: gather_tiles(): flat_grid = donor_grid.reshape(components, extent_x * extent_y * extent_z)]
    all_to_all x2 -> x0, starting transfers between devices: 15.4 us -> none  [the longest x1 10.3 us: local(): lax.all_to_all(corner_send, ('gy', 'gz'), split_axis=1, concat_axis=1, ti...]
    slice x20 -> x0, local copies, waits for them, and re-layouts: 10 us -> none  [the longest x11 5.86 us: padded_2(): lax.slice_in_dim(cells, cells.shape[dim] - width, cells.shape[dim], axis=...]
  transfers between devices with their start and end apart: 32 -> 0, of which waited for: 14 -> 0; matrix products, arithmetic and copies ran while one was open for 4% -> 0% of each run, Pallas kernels for 0% -> 0%
where the time goes in v1:
time: 60 us; the launch traced here: 59.7 us
  Pallas kernels  54.2 us (90%)
  local copies, waits for them, and re-layouts  3.5 us (6%)
  other arithmetic  1.39 us (2%)
  between operations  0.65 us (1%)
    pallas_call x1, Pallas kernels, local(): pl.pallas_call(functools.partial(kernel, (nx, ny, nz, cap)), out_shape=(j...  54.2 us
    unnamed x9, local copies, waits for them, and re-layouts  3.38 us

profile of v1, /device:TPU:0, one launch (start us, length us, event | category | flops | bytes accessed | tf_op | source)
XLA Modules:
  0.0 59.7 jit_solution(6638711365100055465)
XLA Ops:
  0.6 0.7 %convert_element_type.5 = f32[128,3]{0,1:T(4,128)S(1)} convert(s32[128,3]{0,1:T(4,128)} %param.8) | non-fusion elementwise | flops 384 | bytes 3072 | tf_op jit(solution)/shard_map/convert_element_type | solution.py:368
  1.3 0.7 %pad_maximum_fusion = f32[128,18]{0,1:T(8,128)S(1)} fusion(f32[128,15]{0,1:T(8,128)} %param.9, f32[128,3]{0,1:T(4,128)S(1)} %convert_element_type.5), kind=kLoop, calls=%fused_computation | loop fusion | flops 2304 | bytes 18432 | tf_op jit(solution)/shard_map/concatenate | solution.py:368
  2.0 0.0 copy-start.1
  2.0 0.1 copy.10
  2.1 0.0 copy-start.2
  2.2 0.6 %copy-done.2 = s32[128,1]{0,1:T(1,128)S(1)} copy-done((s32[128,1]{0,1:T(1,128)S(1)}, s32[128,1]{0,1:T(1,128)}, u32[]{:S(2)}) %copy-start.2) | copy-done | bytes 536
  2.8 0.1 copy.11.owner
  2.9 0.0 copy-done.1
  2.9 0.0 copy-start
  2.9 1.1 %copy-done = f32[6,16,16,128]{3,2,1,0:T(8,128)S(1)} copy-done((f32[6,16,16,128]{3,2,1,0:T(8,128)S(1)}, f32[6,16,16,128]{3,2,1,0:T(8,128)}, u32[]{:S(2)}) %copy-start) | copy-done | bytes 786456
  4.1 54.2 %shard_map.68 = (f32[6,16,16,128]{3,2,1,0:T(8,128)S(1)}, f32[8,128]{1,0:T(8,128)S(1)}) custom-call(f32[6,16,16,128]{3,2,1,0:T(8,128)S(1)} %copy-done, f32[16,16,128]{2,1,0:T(8,128)S(1)} %copy-done.1, s32[128,1]{1,0:T(8,128)S(1)} %copy.11.owner, f32[128,128]{1,0:T(8,128)S(1)} %pad.4.data), custom_call_target="tpu_custom_call" | custom-call | tf_op jit(solution)/shard_map/pallas_call | solution.py:375
  58.3 0.9 %copy.14 = f32[6,16,16,128]{3,2,1,0:T(8,128)} copy(f32[6,16,16,128]{3,2,1,0:T(8,128)S(1)} %get-tuple-element.8) | data formatting | bytes 1572864
  59.1 0.6 copy.15
  (1 shorter events, 0.0 us)
Async XLA Ops:
  2.0 0.9 %copy-start.1 = (f32[16,16,128]{2,1,0:T(8,128)S(1)}, f32[16,16,128]{2,1,0:T(8,128)}, u32[]{:S(2)}) copy-start(f32[16,16,128]{2,1,0:T(8,128)} %eps.1) | copy-start | bytes 393220
  2.1 0.7 %copy-start.2 = (s32[128,1]{0,1:T(1,128)S(1)}, s32[128,1]{0,1:T(1,128)}, u32[]{:S(2)}) copy-start(s32[128,1]{0,1:T(1,128)} %param.7) | copy-start | bytes 1540
  2.9 1.1 %copy-start = (f32[6,16,16,128]{3,2,1,0:T(8,128)S(1)}, f32[6,16,16,128]{3,2,1,0:T(8,128)}, u32[]{:S(2)}) copy-start(f32[6,16,16,128]{3,2,1,0:T(8,128)} %fields.1) | copy-start | bytes 2359300

commit v2 on v1

--- a/solution.py
+++ b/solution.py
@@ -19,11 +19,20 @@
     return lax.dot_general(a, b, (dims, ((), ())), precision=HI, preferred_element_type=F32)
 
 
+def split(a):
+    hi = a.astype(jnp.bfloat16)
+    return hi, (a - hi.astype(F32)).astype(jnp.bfloat16)
+
+
+def dot16(a, b):
+    return lax.dot_general(a, b, (((1,), (0,)), ((), ())), preferred_element_type=F32)
+
+
 def kernel(
-    sizes, fields, eps, owner, data, out, recept,
+    sizes, fields, eps, owner, bases, weights, out, recept,
     T, F, H, inv, ys, yr, zs, zr, yfs, yfr, zfs, zfr,
-    req, reqr, ans, ansr, W, wz_in, wz_halo, perm,
-    load_sem, send, recv, fsend, frecv, rsend, rrecv, asend, arecv,
+    zfd, DZ, E, data_t, inner, outer, req, reqr, ans, ansr, W, W_lo, wz_in, wz_halo, perm,
+    load_sem, send, recv, fsend, frecv, rsend, rrecv, asend, arecv, dsend, drecv,
 ):
     nx, ny, nz, cap = sizes
     group = ny * nz
@@ -52,7 +61,7 @@
     for lo in (0, y1):
         clear(F.at[:, pl.ds(2, cx), pl.ds(lo, 8)])
         clear(H.at[pl.ds(2, cx), pl.ds(lo, 8)])
-    for ref in (yr, zr, yfr, zfr):
+    for ref in (yr, zr, yfr, zfr, zfd):
         clear(ref)
 
     barrier = pltpu.get_barrier_semaphore()
@@ -73,10 +82,28 @@
         def _():
             pl.semaphore_signal(barrier, inc=1, device_id=dev[side], device_id_type=MESH)
 
-    rows = owner.shape[0]
+    corners = [(sx, sz) for sx in ("xl", "xh") for sz in ("zl", "zh")]
+
+    def corner_dev(sx, sz):
+        return (dev[sx][0], y, dev[sz][2])
+
+    expected = group - 1 + has["xl"].astype(jnp.int32) + has["xh"].astype(jnp.int32)
+    for sx, sz in corners:
+        both = has[sx] & has[sz]
+        expected = expected + both.astype(jnp.int32)
+
+        @pl.when(both)
+        def _():
+            pl.semaphore_signal(barrier, inc=1, device_id=corner_dev(sx, sz), device_id_type=MESH)
+
+    rows = owner.shape[1]
+    data_t[...] = jnp.zeros(data_t.shape, F32)
+    data_t[0:3] = bases[...].astype(F32)
+    data_t[3:18] = weights[...]
+    data_t[18:19] = owner[...].astype(F32)
+    data = jnp.transpose(data_t[...])
     col = lax.broadcasted_iota(jnp.int32, (rows, 128), 1)
-    row = lax.broadcasted_iota(jnp.int32, (rows, 128), 0)
-    own = owner[...]
+    own = data[:, 18:19].astype(jnp.int32)
     hits = (own == col).astype(F32)
     earlier = dot((lax.broadcasted_iota(jnp.int32, (rows, rows), 1)
                    < lax.broadcasted_iota(jnp.int32, (rows, rows), 0)).astype(F32), hits)
@@ -84,7 +111,7 @@
     flat = own * cap + slot
     slots = group * cap
     perm[...] = (flat == lax.broadcasted_iota(jnp.int32, (rows, slots), 1)).astype(F32)
-    packed = dot(perm[...], data[...], ((0,), (0,)))
+    packed = dot(perm[...], data, ((0,), (0,)))
     for o in range(group):
         req[o] = packed[o * cap:(o + 1) * cap]
     reqr[me] = req[me]
@@ -93,7 +120,18 @@
         copy.wait()
     inv[...] = 1.0 / (12.0 * inv[...])
 
-    pl.semaphore_wait(barrier, group - 1 + has["xl"].astype(jnp.int32) + has["xh"].astype(jnp.int32))
+    zi = lax.broadcasted_iota(jnp.int32, (cz, cz), 0)
+    zo = lax.broadcasted_iota(jnp.int32, (cz, cz), 1)
+
+    def stencil(delta):
+        return (jnp.where(delta == -2, 1.0, 0.0) - jnp.where(delta == 2, 1.0, 0.0)
+                + jnp.where(delta == 1, 8.0, 0.0) - jnp.where(delta == -1, 8.0, 0.0))
+
+    inner[...] = stencil(zi - zo).astype(jnp.bfloat16)
+    outer[...] = (stencil(zi - cz - zo) * jnp.where(zi >= cz // 2, 1.0, 0.0)
+                  + stencil(zi + cz - zo) * jnp.where(zi < cz // 2, 1.0, 0.0)).astype(jnp.bfloat16)
+
+    pl.semaphore_wait(barrier, expected)
 
     def remote(src, dst, s, r, target):
         return pltpu.make_async_remote_copy(
@@ -143,13 +181,6 @@
         def _():
             for copy in copies:
                 copy.wait_send()
-
-    def shifts_z(f, edge):
-        lo2 = pltpu.roll(jnp.where(lane >= cz - 2, edge, f), 2, 1)
-        lo1 = pltpu.roll(jnp.where(lane >= cz - 1, edge, f), 1, 1)
-        hi2 = pltpu.roll(jnp.where(lane < 2, edge, f), cz - 2, 1)
-        hi1 = pltpu.roll(jnp.where(lane < 1, edge, f), cz - 1, 1)
-        return (lo2 - hi2) + 8.0 * (hi1 - lo1)
 
     per = cz // 16
 
@@ -182,6 +213,10 @@
             for d in range(1, group):
                 request(d).start()
 
+        for q, c in enumerate(Z_COMPS):
+            hi, lo = split(T[m, c, 2:2 + cx, y0:y1, :].reshape(cx * cy, cz))
+            DZ[q] = (dot16(hi, inner[...]) + dot16(lo, inner[...])).reshape(cx, cy, cz)
+
         for side in ("zl", "zh"):
             finish_recv(z_copies(m, side), side)
         for side in ("yl", "yh"):
@@ -193,8 +228,19 @@
             T[m, c, 2:2 + cx, y1:y1 + 2, :] = yr[m, 0, :, 2 * q:2 * q + 2, :]
         scale = step_size / (m + 1).astype(F32)
 
+        def edges(g, c_):
+            merged = jnp.where(lane % 4 < 2, zr[m, 1, g], zr[m, 0, g])
+            for i in range(per):
+                for q in range(4):
+                    E[q, g * per + i] = pltpu.roll(merged, (2 * cz - (i * 4 + q) * 4 - 2) % cz, 1)
+            return c_
+
+        lax.fori_loop(0, cx // per, edges, 0)
+        for q in range(4):
+            hi, lo = split(E[q].reshape(cx * cy, cz))
+            DZ[q] = DZ[q] + (dot16(hi, outer[...]) + dot16(lo, outer[...])).reshape(cx, cy, cz)
+
         def planes(g, c_):
-            merged = jnp.where(lane % 4 < 2, zr[m, 1, g], zr[m, 0, g])
             for i in range(per):
                 px = 2 + g * per + i
 
@@ -207,9 +253,7 @@
                     return (at(-2) - at(2)) + 8.0 * (at(1) - at(-1))
 
                 def d_z(c):
-                    b = (i * 4 + Z_COMPS.index(c)) * 4
-                    edge = pltpu.roll(merged, (2 * cz - b - 2) % cz, 1)
-                    return shifts_z(T[m, c, px, y0:y1, :], edge)
+                    return DZ[Z_COMPS.index(c), px - 2]
 
                 se = inv[px - 2] * scale
                 sh = scale / 12.0
@@ -240,11 +284,12 @@
         return [remote(F.at[:, pl.ds(lo_src, 2), pl.ds(8, cy)], F.at[:, pl.ds(lo_dst, 2), pl.ds(8, cy)],
                        fsend.at[base], frecv.at[base], dev[side])]
 
-    def xh_copies(side):
-        lo_src, lo_dst = (2, cx + 2) if side == "xl" else (cx, 0)
-        base = 2 if side == "xl" else 3
-        return [remote(H.at[pl.ds(lo_src, 2), pl.ds(8, cy)], H.at[pl.ds(lo_dst, 2), pl.ds(8, cy)],
-                       fsend.at[base], frecv.at[base], dev[side])]
+    last = zfs.shape[0] - 1
+
+    def corner_copy(sx, sz):
+        kx, kz = (0 if sx == "xl" else 1), (0 if sz == "zl" else 1)
+        return remote(zfs.at[0 if sx == "xl" else last], zfd.at[kx, kz],
+                      dsend.at[kx * 2 + kz], drecv.at[kx * 2 + kz], corner_dev(sx, sz))
 
     def yf_copies(side):
         k = 0 if side == "yl" else 1
@@ -267,6 +312,10 @@
         zfs[g] = strip
     for side in ("zl", "zh"):
         start(zf_copies(side), side)
+    for sx, sz in corners:
+        @pl.when(has[sx] & has[sz])
+        def _():
+            corner_copy(sx, sz).start()
 
     for d in range(1, group):
         request(d).wait_recv()
@@ -287,7 +336,8 @@
     yrows = F.shape[2]
     for lo in range(0, W.shape[1], 128):
         li = lo + lax.broadcasted_iota(jnp.int32, (slots, 128), 1)
-        W[:, lo:lo + 128] = spread(li // yrows - bx, 3) * spread(li % yrows - 6 - by, 8)
+        both_xy = spread(li // yrows - bx, 3) * spread(li % yrows - 6 - by, 8)
+        W[:, lo:lo + 128], W_lo[:, lo:lo + 128] = split(both_xy)
     li = lax.broadcasted_iota(jnp.int32, (slots, cz), 1)
     wz_in[...] = spread(li + 2 - bz, 13)
     tail = li % 4
@@ -299,11 +349,17 @@
         merged = jnp.where(lane % 4 < 2, zfr[1, g], zfr[0, g])
         for i in range(wide):
             H[2 + g * wide + i, y0:y1, :] = pltpu.roll(merged, (cz - i * 32) % cz, 1) if i else merged
-    for side in ("xl", "xh"):
-        start(xh_copies(side), side)
+    for sx, sz in corners:
+        @pl.when(has[opposite[sx]] & has[opposite[sz]])
+        def _():
+            corner_copy(sx, sz).wait_recv()
+    for kx, at, shift in ((1, 0, (wide - 2) * 32), (0, cx + 2, 0)):
+        merged = jnp.where(lane % 4 < 2, zfd[kx, 1], zfd[kx, 0])
+        for i in range(2):
+            move = (cz - shift - i * 32) % cz
+            H[at + i, y0:y1, :] = pltpu.roll(merged, move, 1) if move else merged
     for side in ("xl", "xh"):
         finish_recv(xf_copies(side), side)
-        finish_recv(xh_copies(side), side)
     for k, lo in ((0, y0), (1, y1 - 2)):
         for c in range(6):
             yfs[k, :, 2 * c:2 * c + 2, :] = F[c, :, lo:lo + 2, :]
@@ -318,12 +374,18 @@
         H[:, lo:lo + 2, :] = yfr[k, :, 12:14, :]
 
     depth = W.shape[1]
-    halo = dot(W[...], H[...].reshape(depth, cz)) * wz_halo[...]
+
+    def apply(block):
+        hi, lo = split(block)
+        return dot16(W[...], hi) + dot16(W[...], lo) + dot16(W_lo[...], hi)
+
+    halo = apply(H[...].reshape(depth, cz)) * wz_halo[...]
     result = jnp.zeros((slots, cz), F32)
-    for c in range(6):
-        part = dot(W[...], F[c].reshape(depth, cz)) * wz_in[...]
-        part = part + jnp.where(li // 4 == c, halo, 0.0)
-        result = jnp.where(li == c, jnp.sum(part, axis=1, keepdims=True), result)
+    for c in range(0, 6, 2):
+        pair = apply(jnp.concatenate([F[c].reshape(depth, cz), F[c + 1].reshape(depth, cz)], axis=1))
+        for k in range(2):
+            part = pair[:, k * cz:(k + 1) * cz] * wz_in[...] + jnp.where(li // 4 == c + k, halo, 0.0)
+            result = jnp.where(li == c + k, jnp.sum(part, axis=1, keepdims=True), result)
     for o in range(group):
         ans[o] = result[o * cap:(o + 1) * cap]
     for d in range(1, group):
@@ -336,7 +398,7 @@
     else:
         got = jnp.concatenate([ansr[o] for o in range(group)], axis=0)
     picked = dot(perm[...], got)
-    recept[...] = jnp.transpose(picked)[0:8, :]
+    recept[...] = jnp.transpose(picked)[0:6, :]
 
     store.wait()
     for m in range(4):
@@ -348,11 +410,14 @@
             finish_send(z_copies(m, side), side)
     for side in ("xl", "xh"):
         finish_send(xf_copies(side), side)
-        finish_send(xh_copies(side), side)
     for side in ("yl", "yh"):
         finish_send(yf_copies(side), side)
     for side in ("zl", "zh"):
         finish_send(zf_copies(side), side)
+    for sx, sz in corners:
+        @pl.when(has[sx] & has[sz])
+        def _():
+            corner_copy(sx, sz).wait_send()
     for d in range(1, group):
         request(d).wait_send()
         answer(d).wait_send()
@@ -365,22 +430,20 @@
     group = ny * nz
     cap = 2 * rows // group
     slots = group * cap
-    data = jnp.concatenate([donor_base.astype(F32), donor_weights], axis=1)
-    data = jnp.pad(data, ((0, 0), (0, 128 - data.shape[1])))
     vmem = pltpu.VMEM
     dma = pltpu.SemaphoreType.DMA
     yrows = cy + 16
     depth = (cx + 4) * yrows
-    depth_pad = depth
     out, recept = pl.pallas_call(
         functools.partial(kernel, (nx, ny, nz, cap)),
         out_shape=(
             jax.ShapeDtypeStruct(fields.shape, F32),
-            jax.ShapeDtypeStruct((8, rows), F32),
+            jax.ShapeDtypeStruct((6, rows), F32),
         ),
         in_specs=[
             pl.BlockSpec(memory_space=pl.ANY),
             pl.BlockSpec(memory_space=pl.ANY),
+            pl.BlockSpec(memory_space=vmem),
             pl.BlockSpec(memory_space=vmem),
             pl.BlockSpec(memory_space=vmem),
         ],
@@ -398,11 +461,18 @@
             vmem((2, cx + 4, 16, cz), F32),
             vmem((cx * 32 // cz, cy, cz), F32),
             vmem((2, cx * 32 // cz, cy, cz), F32),
+            vmem((2, 2, cy, cz), F32),
+            vmem((4, cx, cy, cz), F32),
+            vmem((4, cx, cy, cz), F32),
+            vmem((128, rows), F32),
+            vmem((cz, cz), jnp.bfloat16),
+            vmem((cz, cz), jnp.bfloat16),
             vmem((group, cap, 128), F32),
             vmem((group, cap, 128), F32),
             vmem((group, cap, 128), F32),
             vmem((group, cap, 128), F32),
-            vmem((slots, depth_pad), F32),
+            vmem((slots, depth), jnp.bfloat16),
+            vmem((slots, depth), jnp.bfloat16),
             vmem((slots, cz), F32),
             vmem((slots, cz), F32),
             vmem((rows, slots), F32),
@@ -415,12 +485,14 @@
             dma((group,)),
             dma((group,)),
             dma((group,)),
+            dma((4,)),
+            dma((4,)),
         ],
         compiler_params=pltpu.CompilerParams(
             collective_id=0, has_side_effects=True, vmem_limit_bytes=40 * 1024 * 1024
         ),
-    )(fields, permittivity, donor_owner, data)
-    return out, recept[0:6]
+    )(fields, permittivity, donor_owner.T, donor_base.T, donor_weights.T)
+    return out, recept
 
 
 def solution(mesh):

time: 60 us -> 45.7 us (0.76)
  Pallas kernels: 54.2 us -> 40 us
  other arithmetic: 1.39 us -> 0 us
  local copies, waits for them, and re-layouts: 3.5 us -> 4.88 us
    pallas_call x1, Pallas kernels: 54.2 us -> 40 us  [local(): pl.pallas_call(functools.partial(kernel, (nx, ny, nz, cap)), out_shape=(j...]
    unnamed x9 -> x12, local copies, waits for them, and re-layouts: 3.38 us -> 4.88 us
    concatenate x1 -> x0, other arithmetic: 0.7 us -> none  [local(): data = jnp.concatenate([donor_base.astype(F32), donor_weights], axis=1)]
    convert_element_type x1 -> x0, other arithmetic: 0.68 us -> none  [local(): data = jnp.concatenate([donor_base.astype(F32), donor_weights], axis=1)]
where the time goes in v2:
time: 45.7 us; the launch traced here: 45.5 us
  Pallas kernels  40 us (88%)
  local copies, waits for them, and re-layouts  4.88 us (11%)
  between operations  0.66 us (1%)
    pallas_call x1, Pallas kernels, local(): pl.pallas_call(functools.partial(kernel, (nx, ny, nz, cap)), out_shape=(j...  40 us
    unnamed x12, local copies, waits for them, and re-layouts  4.88 us

profile of v2, /device:TPU:0, one launch (start us, length us, event | category | flops | bytes accessed | tf_op | source)
XLA Modules:
  0.0 45.5 jit_solution(9070231925966385643)
XLA Ops:
  0.6 0.0 copy-start.3
  0.6 0.0 copy-start.4
  0.7 0.7 %copy-done.3 = s32[128,3]{0,1:T(4,128)S(1)} copy-done((s32[128,3]{0,1:T(4,128)S(1)}, s32[128,3]{0,1:T(4,128)}, u32[]{:S(2)}) %copy-start.3) | copy-done | bytes 1560
  1.3 0.0 copy-done.4
  1.3 0.0 copy-start
  1.3 1.1 %copy-done = f32[6,16,16,128]{3,2,1,0:T(8,128)S(1)} copy-done((f32[6,16,16,128]{3,2,1,0:T(8,128)S(1)}, f32[6,16,16,128]{3,2,1,0:T(8,128)}, u32[]{:S(2)}) %copy-start) | copy-done | bytes 786456
  2.5 0.0 copy-start.1
  2.5 0.9 %copy-done.1 = f32[16,16,128]{2,1,0:T(8,128)S(1)} copy-done((f32[16,16,128]{2,1,0:T(8,128)S(1)}, f32[16,16,128]{2,1,0:T(8,128)}, u32[]{:S(2)}) %copy-start.1) | copy-done | bytes 131096
  3.4 0.0 copy-start.2
  3.4 0.7 %copy-done.2 = f32[128,15]{0,1:T(8,128)S(1)} copy-done((f32[128,15]{0,1:T(8,128)S(1)}, f32[128,15]{0,1:T(8,128)}, u32[]{:S(2)}) %copy-start.2) | copy-done | bytes 7704
  4.1 40.0 %shard_map.68 = (f32[6,16,16,128]{3,2,1,0:T(8,128)S(1)}, f32[6,128]{1,0:T(8,128)S(1)}) custom-call(f32[6,16,16,128]{3,2,1,0:T(8,128)S(1)} %copy-done, f32[16,16,128]{2,1,0:T(8,128)S(1)} %copy-done.1, s32[1,128]{1,0:T(1,128)S(1)} %bitcast.5, s32[3,128]{1,0:T(4,128)S(1)} %bitcast.4, f32[15,128]{1,0:T(8,128)S(1)} %bitcast.3), custom_call_target="tpu_custom_call" | custom-call | tf_op jit(solution)/shard_map/pallas_call | solution.py:437
  44.0 0.9 %copy.9 = f32[6,16,16,128]{3,2,1,0:T(8,128)} copy(f32[6,16,16,128]{3,2,1,0:T(8,128)S(1)} %get-tuple-element.4) | data formatting | bytes 1572864
  44.9 0.6 %copy.10 = f32[6,128]{1,0:T(8,128)} copy(f32[6,128]{1,0:T(8,128)S(1)} %get-tuple-element.5) | data formatting | bytes 6144
Async XLA Ops:
  0.6 0.7 %copy-start.3 = (s32[128,3]{0,1:T(4,128)S(1)}, s32[128,3]{0,1:T(4,128)}, u32[]{:S(2)}) copy-start(s32[128,3]{0,1:T(4,128)} %param.8) | copy-start | bytes 4612
  0.6 0.7 %copy-start.4 = (s32[128,1]{0,1:T(1,128)S(1)}, s32[128,1]{0,1:T(1,128)}, u32[]{:S(2)}) copy-start(s32[128,1]{0,1:T(1,128)} %param.7) | copy-start | bytes 1540
  1.3 1.1 %copy-start = (f32[6,16,16,128]{3,2,1,0:T(8,128)S(1)}, f32[6,16,16,128]{3,2,1,0:T(8,128)}, u32[]{:S(2)}) copy-start(f32[6,16,16,128]{3,2,1,0:T(8,128)} %fields.1) | copy-start | bytes 2359300
  2.5 0.9 %copy-start.1 = (f32[16,16,128]{2,1,0:T(8,128)S(1)}, f32[16,16,128]{2,1,0:T(8,128)}, u32[]{:S(2)}) copy-start(f32[16,16,128]{2,1,0:T(8,128)} %eps.1) | copy-start | bytes 393220
  3.4 0.7 %copy-start.2 = (f32[128,15]{0,1:T(8,128)S(1)}, f32[128,15]{0,1:T(8,128)}, u32[]{:S(2)}) copy-start(f32[128,15]{0,1:T(8,128)} %param.9) | copy-start | bytes 23044
